TPU v7x, 32 devices: a whole 2x2x4 slice. The times are simulated.
32 devices in a mesh: mode: 8 (over z, y), cores: 4 (over x, core).
Axes of the slice: x: 2, y: 2, z: 4, core: 2. Of those that a mesh axis runs over, the one named last changes fastest.
Arguments:
- train_cores: bfloat16 [4, 400, 32, 400], P('cores', None, 'mode'), may hold values from -0.24748737 to 0.24748737
- sketch_cores: bfloat16 [4, 100, 32, 100], P('cores', None, 'mode'), may hold values from -0.3125 to 0.3125
- left_interface: float32 [100, 400], replicated, may hold values from -6 to 6
- right_sketch: bfloat16 [400, 100], replicated, may hold values from -6 to 6
Outputs:
- frames: bfloat16 [4, 100, 32, 100], P('cores', None, 'mode')
- interfaces: float32 [4, 100, 400], P('cores')
All inputs are finite; a program needn't handle non-finite values.
Results may differ from a plain program's by a relative error of at most 0.019.
Values may be sent and summed in bfloat16 or wider, within the bound.
A program may use at most 64 MiB of HBM per device.

v0:
```python
import math
import jax
import jax.numpy as jnp
from jax import lax
from jax.sharding import PartitionSpec as P


def from_behind(shard, axis, by):
    size = lax.axis_size(axis)
    pairs = [(i, i + by) for i in range(size) if 0 <= i + by < size]
    return lax.ppermute(shard, axis, pairs)


def body(train_cores, sketch_cores, left_interface, right_sketch):
    my_core = train_cores[0]
    my_sketch = sketch_cores[0]
    rank_size = my_core.shape[0]
    mode_local = my_core.shape[1]
    sketch_size = my_sketch.shape[0]
    group_index = lax.axis_index("cores")
    group_count = lax.axis_size("cores")
    final_group = group_count - 1
    flat_core = my_core.reshape(rank_size * mode_local, rank_size)
    sketch_flat = my_sketch.reshape(sketch_size, mode_local * sketch_size)
    sketch = right_sketch
    for round_index in range(group_count - 1):
        partial_value = jnp.dot(flat_core, sketch, preferred_element_type=jnp.float32).astype(
            jnp.bfloat16
        )
        partial_value = partial_value.reshape(rank_size, mode_local * sketch_size)
        local_term = lax.dot_general(
            partial_value, sketch_flat, (((1,), (1,)), ((), ())), preferred_element_type=jnp.float32
        )
        summed = lax.psum(local_term, "mode")
        received = from_behind(summed.astype(jnp.bfloat16), "cores", -1)
        sketch = jnp.where(group_index == final_group, right_sketch, received)
    frame_scale = math.sqrt(sketch_size * mode_local * lax.axis_size("mode"))
    wide_core = my_core.reshape(rank_size, mode_local * rank_size)
    interface = left_interface
    for round_index in range(group_count):
        carry_low = interface.astype(jnp.bfloat16)
        built = jnp.dot(carry_low, wide_core, preferred_element_type=jnp.float32)
        built = built.astype(jnp.bfloat16).reshape(sketch_size * mode_local, rank_size)
        images = jnp.dot(built, sketch, preferred_element_type=jnp.float32)
        core_local = lax.dot_general(
            built, built, (((0,), (0,)), ((), ())), preferred_element_type=jnp.float32
        )
        core_square = lax.psum(core_local, "mode")
        sketch_wide = sketch.astype(jnp.float32)
        projected = lax.dot_general(
            sketch_wide, core_square, (((0,), (0,)), ((), ())), precision=lax.Precision.HIGHEST
        )
        gram_matrix = jnp.dot(projected, sketch_wide, precision=lax.Precision.HIGHEST)
        chol_lower = jnp.linalg.cholesky(gram_matrix)
        frame_rows = lax.linalg.triangular_solve(chol_lower, images.T, left_side=True, lower=True)
        next_interface = lax.linalg.triangular_solve(
            chol_lower, projected, left_side=True, lower=True
        )
        frame_out = (frame_rows.T * frame_scale).astype(jnp.bfloat16)
        interface_out = next_interface
        if round_index < group_count - 1:
            passed = from_behind(next_interface.astype(jnp.bfloat16), "cores", 1)
            interface = jnp.where(group_index == 0, left_interface, passed.astype(jnp.float32))
    frames = frame_out.reshape(1, sketch_size, mode_local, sketch_size)
    interfaces = interface_out.reshape(1, sketch_size, rank_size)
    return (frames, interfaces)


def solution(mesh):
    in_specs = (P("cores", None, "mode", None), P("cores", None, "mode", None), P(), P())
    out_specs = (P("cores", None, "mode", None), P("cores", None, None))
    return jax.shard_map(body, mesh=mesh, in_specs=in_specs, out_specs=out_specs, check_vma=False)
```

profile of v0, /device:TPU:0, one launch (start us, length us, event | category | flops | bytes accessed | tf_op | source)
XLA Modules:
  0.0 529.6 jit_solution(15847679337264826134)
XLA Ops:
  7.2 2.8 reshape_squeeze.9
  11.7 42.0 %all-reduce.15 = bf16[400,100]{1,0:T(8,128)(2,1)} all-reduce(f32[400,100]{1,0:T(8,128)S(1)} %fusion.30), channel_id=1, replica_groups=mesh['mode'=8,'cores'=4] {'mode'}, use_global_device_ids=true, to_apply=%region_0.0 | all-reduce | flops 40000 | bytes 240000 | tf_op jit(solution)/shard_map/psum | solution.py:34
  55.1 3.4 reshape_squeeze.11
  61.2 2.3 fusion
  65.4 2.1 reshape.43
  67.5 2.0 fusion.31
  69.4 36.3 %all-reduce.16 = bf16[400,100]{1,0:T(8,128)(2,1)} all-reduce(f32[400,100]{1,0:T(8,128)} %fusion.31), channel_id=1, replica_groups=mesh['mode'=8,'cores'=4] {'mode'}, use_global_device_ids=true, to_apply=%region_1.2 | all-reduce | flops 40000 | bytes 240000 | tf_op jit(solution)/shard_map/psum | solution.py:34
  112.0 40.1 %all-reduce.17 = bf16[400,100]{1,0:T(8,128)(2,1)S(1)} all-reduce(f32[400,100]{1,0:T(8,128)S(1)} %fusion.32), channel_id=1, replica_groups=mesh['mode'=8,'cores'=4] {'mode'}, use_global_device_ids=true, to_apply=%region_2.3 | all-reduce | flops 40000 | bytes 240000 | tf_op jit(solution)/shard_map/psum | solution.py:34
  155.4 31.4 %all-reduce.8.cloned.1.call-done = f32[400,400]{1,0:T(8,128)} async-done(((f32[400,400]{1,0:T(8,128)}), f32[400,400]{1,0:T(8,128)}) %all-reduce.8.cloned.1.call-update) | async-done | bytes 640016 | tf_op jit(solution)/shard_map/psum | solution.py:48
  186.9 2.1 fusion.34
  189.5 9.1 %cholesky.74 = f32[100,100]{1,0:T(8,128)S(1)} custom-call(f32[100,100]{1,0:T(8,128)S(1)} %fusion.23), custom_call_target="Cholesky" | custom-call | tf_op jit(solution)/shard_map/jit(cholesky)/cholesky | solution.py:54
  200.0 7.7 %custom-call.9 = f32[1,100,100]{1,2,0:T(8,128)S(1)} custom-call(f32[1,100,100]{2,1,0:T(8,128)S(1)} %fusion.11), custom_call_target="InvertDiagBlocksLowerTriangular" | custom-call | tf_op jit(solution)/shard_map/triangular_solve/custom-call.0 | solution.py:56
  212.5 78.7 %all-reduce.10.cloned.1.call-done = f32[400,400]{1,0:T(8,128)} async-done(((f32[400,400]{1,0:T(8,128)}), f32[400,400]{1,0:T(8,128)}) %all-reduce.10.cloned.1.call-update) | async-done | bytes 640016 | tf_op jit(solution)/shard_map/psum | solution.py:48
  291.2 2.1 fusion.37
  293.9 9.1 %cholesky.85 = f32[100,100]{1,0:T(8,128)S(1)} custom-call(f32[100,100]{1,0:T(8,128)S(1)} %fusion.21), custom_call_target="Cholesky" | custom-call | tf_op jit(solution)/shard_map/jit(cholesky)/cholesky | solution.py:54
  304.4 7.7 %custom-call.10 = f32[1,100,100]{1,2,0:T(8,128)S(1)} custom-call(f32[1,100,100]{2,1,0:T(8,128)S(1)} %fusion.12), custom_call_target="InvertDiagBlocksLowerTriangular" | custom-call | tf_op jit(solution)/shard_map/triangular_solve/custom-call.0 | solution.py:56
  317.1 78.5 %all-reduce.12.cloned.1.call-done = f32[400,400]{1,0:T(8,128)} async-done(((f32[400,400]{1,0:T(8,128)}), f32[400,400]{1,0:T(8,128)}) %all-reduce.12.cloned.1.call-update) | async-done | bytes 640016 | tf_op jit(solution)/shard_map/psum | solution.py:48
  395.6 2.1 fusion.40
  398.2 9.1 %cholesky.96 = f32[100,100]{1,0:T(8,128)S(1)} custom-call(f32[100,100]{1,0:T(8,128)S(1)} %fusion.19), custom_call_target="Cholesky" | custom-call | tf_op jit(solution)/shard_map/jit(cholesky)/cholesky | solution.py:54
  408.7 7.7 %custom-call.11 = f32[1,100,100]{1,2,0:T(8,128)S(1)} custom-call(f32[1,100,100]{2,1,0:T(8,128)S(1)} %fusion.13), custom_call_target="InvertDiagBlocksLowerTriangular" | custom-call | tf_op jit(solution)/shard_map/triangular_solve/custom-call.0 | solution.py:56
  421.5 78.5 %all-reduce.14.cloned.1.call-done = f32[400,400]{1,0:T(8,128)} async-done(((f32[400,400]{1,0:T(8,128)}), f32[400,400]{1,0:T(8,128)}) %all-reduce.14.cloned.1.call-update) | async-done | bytes 640016 | tf_op jit(solution)/shard_map/psum | solution.py:48
  499.9 2.1 fusion.43
  502.6 9.1 %cholesky.107 = f32[100,100]{1,0:T(8,128)S(1)} custom-call(f32[100,100]{1,0:T(8,128)S(1)} %fusion.17), custom_call_target="Cholesky" | custom-call | tf_op jit(solution)/shard_map/jit(cholesky)/cholesky | solution.py:54
  513.0 7.7 %custom-call.12 = f32[1,100,100]{1,2,0:T(8,128)S(1)} custom-call(f32[1,100,100]{2,1,0:T(8,128)S(1)} %fusion.14), custom_call_target="InvertDiagBlocksLowerTriangular" | custom-call | tf_op jit(solution)/shard_map/triangular_solve/custom-call.0 | solution.py:55
  (88 shorter events, 41.7 us)
Async XLA Ops:
  7.2 2.9 copy-start.4
  7.2 179.7 %all-reduce.8.cloned.1.call-start = ((), (), s32[]{:S(2)}) async-start(), calls=%async_computation | async-start | bytes 1638400 | tf_op jit(solution)/shard_map/psum | solution.py:48
  10.1 1.2 copy-start.6
  11.4 42.3 %copy-start.2 = (bf16[100,400]{1,0:T(8,128)(2,1)}, bf16[100,400]{1,0:T(8,128)(2,1)S(1)}, u32[]{:S(2)}) copy-start(bf16[100,400]{1,0:T(8,128)(2,1)S(1)} %reshape.69) | copy-start | bytes 240004
  53.7 4.8 copy-start
  53.7 7.5 %collective-permute-start = (bf16[400,100]{1,0:T(8,128)(2,1)}, bf16[400,100]{1,0:T(8,128)(2,1)}, u32[]{:S(2)}, u32[]{:S(2)}) collective-permute-start(bf16[400,100]{1,0:T(8,128)(2,1)} %all-reduce.15), channel_id=1, source_target_pairs={{1,0},{2,1},{3,2},{5,4},{6,5},{7,6},{9,8},{10,9},{11,10},{13,12},{... | collective-permute-start | bytes 240008 | tf_op jit(solution)/shard_map/ppermute | solution.py:11
  105.7 3.5 collective-permute-start.1
  108.4 182.9 %all-reduce.10.cloned.1.call-start = ((), (), s32[]{:S(2)}) async-start(), calls=%async_computation.1 | async-start | bytes 1638400 | tf_op jit(solution)/shard_map/psum | solution.py:48
  110.8 0.9 copy-start.3
  110.8 44.6 %copy-start.5 = (bf16[400,100]{1,0:T(8,128)(2,1)S(1)}, bf16[400,100]{1,0:T(8,128)(2,1)}, u32[]{:S(2)}) copy-start(bf16[400,100]{1,0:T(8,128)(2,1)} %param.10) | copy-start | bytes 240004
  152.1 58.2 %copy-start.1 = (f32[100,400]{0,1:T(8,128)S(1)}, f32[100,400]{0,1:T(8,128)}, u32[]{:S(2)}) copy-start(f32[100,400]{0,1:T(8,128)} %param.9) | copy-start | bytes 480004
  152.1 3.3 collective-permute-start.2
  208.0 2.2 collective-permute-start.3
  212.5 183.1 %all-reduce.12.cloned.1.call-start = ((), (), s32[]{:S(2)}) async-start(), calls=%async_computation.2 | async-start | bytes 1638400 | tf_op jit(solution)/shard_map/psum | solution.py:48
  312.4 2.5 collective-permute-start.4
  317.1 182.9 %all-reduce.14.cloned.1.call-start = ((), (), s32[]{:S(2)}) async-start(), calls=%async_computation.3 | async-start | bytes 1638400 | tf_op jit(solution)/shard_map/psum | solution.py:48
  416.7 2.2 collective-permute-start.5
Sparse Core Ops, SparseCore 0:
  108.5 78.3 all-reduce.7
  212.6 78.5 all-reduce.9
  317.2 78.3 all-reduce.11
  421.3 78.5 all-reduce.13
where the time goes:
time: 531 us; the launch traced here: 530 us
  waiting for transfers between devices  272 us (51%)
  blocking collectives  118 us (22%)
  other arithmetic  72.6 us (14%)
  matrix products  27.2 us (5%)
  local copies, waits for them, and re-layouts  16 us (3%)
  between operations  14.3 us (3%)
  starting transfers between devices  8.83 us (2%)
    psum x4, waiting for transfers between devices, body(): core_square = lax.psum(core_local, 'mode')  267 us
    psum x3, blocking collectives, body(): summed = lax.psum(local_term, 'mode')  118 us
    another operation x12, other arithmetic, body(): chol_lower = jnp.linalg.cholesky(gram_matrix)  39.3 us
    another operation x6, other arithmetic, body(): lax.linalg.triangular_solve(chol_lower, projected, left_side=True, lower=...  25 us
  transfers between devices with their start and end apart: 10, of which 9 were waited for; matrix products, arithmetic and copies ran while one was open for 2% of the time, Pallas kernels for 0%

commit v1 on v0

--- a/solution.py
+++ b/solution.py
@@ -31,7 +31,8 @@
         local_term = lax.dot_general(
             partial_value, sketch_flat, (((1,), (1,)), ((), ())), preferred_element_type=jnp.float32
         )
-        summed = lax.psum(local_term, "mode")
+        shards = lax.all_gather(local_term, "mode")
+        summed = jnp.sum(shards, axis=0)
         received = from_behind(summed.astype(jnp.bfloat16), "cores", -1)
         sketch = jnp.where(group_index == final_group, right_sketch, received)
     frame_scale = math.sqrt(sketch_size * mode_local * lax.axis_size("mode"))

time: 531 us -> 584 us (1.100)
  waiting for transfers between devices: 272 us -> 450 us
  blocking collectives: 118 us -> 0 us
  local copies, waits for them, and re-layouts: 16 us -> 9.42 us
    all_gather x0 -> x3, waiting for transfers between devices: none -> 133 us  [body(): shards = lax.all_gather(local_term, 'mode')]
    psum x3 -> x0, blocking collectives: 118 us -> none  [body(): summed = lax.psum(local_term, 'mode')]
    psum x4, waiting for transfers between devices: 267 us -> 308 us  [body(): core_square = lax.psum(core_local, 'mode')]
  transfers between devices with their start and end apart: 10 -> 13, of which waited for: 9 -> 13; matrix products, arithmetic and copies ran while one was open for 2% -> 1% of each run, Pallas kernels for 0% -> 0%
where the time goes in v1:
time: 584 us
  waiting for transfers between devices  450 us (77%)
  other arithmetic  77.3 us (13%)
  matrix products  24.4 us (4%)
  between operations  14.6 us (2%)
  local copies, waits for them, and re-layouts  9.42 us (2%)
  starting transfers between devices  8.45 us (1%)
    psum x4, waiting for transfers between devices, body(): core_square = lax.psum(core_local, 'mode')  308 us
    all_gather x3, waiting for transfers between devices, body(): shards = lax.all_gather(local_term, 'mode')  133 us
    another operation x12, other arithmetic, body(): chol_lower = jnp.linalg.cholesky(gram_matrix)  39.3 us
    another operation x6, other arithmetic, body(): lax.linalg.triangular_solve(chol_lower, projected, left_side=True, lower=...  25 us
  transfers between devices with their start and end apart: 13, of which 13 were waited for; matrix products, arithmetic and copies ran while one was open for 1% of the time, Pallas kernels for 0%

profile of v1, /device:TPU:0, one launch (start us, length us, event | category | flops | bytes accessed | tf_op | source)
XLA Modules:
  0.0 583.8 jit_solution(4911555481705809838)
XLA Ops:
  7.2 2.8 reshape_squeeze.9
  12.4 47.7 %all-gather.7.cloned.1.call-done = f32[3200,100]{1,0:T(8,128)} async-done(((f32[400,100]{1,0:T(8,128)}), f32[3200,100]{1,0:T(8,128)}) %all-gather.7.cloned.1.call-update) | async-done | bytes 1280016 | tf_op jit(solution)/shard_map/all_gather | solution.py:34
  62.9 1.9 collective-permute-done
  67.1 44.7 %all-gather.9.cloned.1.call-done = f32[3200,100]{1,0:T(8,128)} async-done(((f32[400,100]{1,0:T(8,128)}), f32[3200,100]{1,0:T(8,128)}) %all-gather.9.cloned.1.call-update) | async-done | bytes 1280016 | tf_op jit(solution)/shard_map/all_gather | solution.py:34
  114.6 1.9 collective-permute-done.1
  118.8 1.6 reshape_squeeze.11
  122.7 40.8 %all-gather.11.cloned.1.call-done = f32[3200,100]{1,0:T(8,128)} async-done(((f32[400,100]{1,0:T(8,128)}), f32[3200,100]{1,0:T(8,128)}) %all-gather.11.cloned.1.call-update) | async-done | bytes 1280016 | tf_op jit(solution)/shard_map/all_gather | solution.py:34
  166.3 1.9 collective-permute-done.2
  168.2 72.5 %all-reduce.5.cloned.1.call-done = f32[400,400]{1,0:T(8,128)} async-done(((f32[400,400]{1,0:T(8,128)}), f32[400,400]{1,0:T(8,128)}) %all-reduce.5.cloned.1.call-update) | async-done | bytes 640016 | tf_op jit(solution)/shard_map/psum | solution.py:49
  240.7 2.1 fusion.34
  243.3 9.1 %cholesky.74 = f32[100,100]{1,0:T(8,128)S(1)} custom-call(f32[100,100]{1,0:T(8,128)S(1)} %fusion.23), custom_call_target="Cholesky" | custom-call | tf_op jit(solution)/shard_map/jit(cholesky)/cholesky | solution.py:55
  253.8 7.7 %custom-call.9 = f32[1,100,100]{1,2,0:T(8,128)S(1)} custom-call(f32[1,100,100]{2,1,0:T(8,128)S(1)} %fusion.11), custom_call_target="InvertDiagBlocksLowerTriangular" | custom-call | tf_op jit(solution)/shard_map/triangular_solve/custom-call.0 | solution.py:57
  266.4 78.7 %all-reduce.7.cloned.1.call-done = f32[400,400]{1,0:T(8,128)} async-done(((f32[400,400]{1,0:T(8,128)}), f32[400,400]{1,0:T(8,128)}) %all-reduce.7.cloned.1.call-update) | async-done | bytes 640016 | tf_op jit(solution)/shard_map/psum | solution.py:49
  345.1 2.1 fusion.37
  347.7 9.1 %cholesky.85 = f32[100,100]{1,0:T(8,128)S(1)} custom-call(f32[100,100]{1,0:T(8,128)S(1)} %fusion.21), custom_call_target="Cholesky" | custom-call | tf_op jit(solution)/shard_map/jit(cholesky)/cholesky | solution.py:55
  358.2 7.7 %custom-call.10 = f32[1,100,100]{1,2,0:T(8,128)S(1)} custom-call(f32[1,100,100]{2,1,0:T(8,128)S(1)} %fusion.12), custom_call_target="InvertDiagBlocksLowerTriangular" | custom-call | tf_op jit(solution)/shard_map/triangular_solve/custom-call.0 | solution.py:57
  370.7 78.7 %all-reduce.9.cloned.1.call-done = f32[400,400]{1,0:T(8,128)} async-done(((f32[400,400]{1,0:T(8,128)}), f32[400,400]{1,0:T(8,128)}) %all-reduce.9.cloned.1.call-update) | async-done | bytes 640016 | tf_op jit(solution)/shard_map/psum | solution.py:49
  449.4 2.1 fusion.40
  452.0 9.1 %cholesky.96 = f32[100,100]{1,0:T(8,128)S(1)} custom-call(f32[100,100]{1,0:T(8,128)S(1)} %fusion.19), custom_call_target="Cholesky" | custom-call | tf_op jit(solution)/shard_map/jit(cholesky)/cholesky | solution.py:55
  462.5 7.7 %custom-call.11 = f32[1,100,100]{1,2,0:T(8,128)S(1)} custom-call(f32[1,100,100]{2,1,0:T(8,128)S(1)} %fusion.13), custom_call_target="InvertDiagBlocksLowerTriangular" | custom-call | tf_op jit(solution)/shard_map/triangular_solve/custom-call.0 | solution.py:57
  475.3 78.5 %all-reduce.11.cloned.1.call-done = f32[400,400]{1,0:T(8,128)} async-done(((f32[400,400]{1,0:T(8,128)}), f32[400,400]{1,0:T(8,128)}) %all-reduce.11.cloned.1.call-update) | async-done | bytes 640016 | tf_op jit(solution)/shard_map/psum | solution.py:49
  553.8 2.1 fusion.43
  556.4 9.1 %cholesky.107 = f32[100,100]{1,0:T(8,128)S(1)} custom-call(f32[100,100]{1,0:T(8,128)S(1)} %fusion.17), custom_call_target="Cholesky" | custom-call | tf_op jit(solution)/shard_map/jit(cholesky)/cholesky | solution.py:55
  566.9 7.7 %custom-call.12 = f32[1,100,100]{1,2,0:T(8,128)S(1)} custom-call(f32[1,100,100]{2,1,0:T(8,128)S(1)} %fusion.14), custom_call_target="InvertDiagBlocksLowerTriangular" | custom-call | tf_op jit(solution)/shard_map/triangular_solve/custom-call.0 | solution.py:56
  (91 shorter events, 41.9 us)
Async XLA Ops:
  7.2 2.9 copy-start.2
  7.2 52.9 %all-gather.7.cloned.1.call-start = ((), (), s32[]{:S(2)}) async-start(), calls=%async_computation.4 | async-start | bytes 1843200 | tf_op jit(solution)/shard_map/all_gather | solution.py:34
  10.1 1.2 copy-start.3
  12.4 99.4 %all-gather.9.cloned.1.call-start = ((), (), s32[]{:S(2)}) async-start(), calls=%async_computation.5 | async-start | bytes 1843200 | tf_op jit(solution)/shard_map/all_gather | solution.py:34
  61.6 3.2 collective-permute-start
  67.0 96.4 %all-gather.11.cloned.1.call-start = ((), (), s32[]{:S(2)}) async-start(), calls=%async_computation.6 | async-start | bytes 1843200 | tf_op jit(solution)/shard_map/all_gather | solution.py:34
  113.3 3.2 collective-permute-start.1
  117.2 1.6 copy-start
  118.7 1.7 copy-start.1
  118.7 122.0 %all-reduce.5.cloned.1.call-start = ((), (), s32[]{:S(2)}) async-start(), calls=%async_computation | async-start | bytes 1638400 | tf_op jit(solution)/shard_map/psum | solution.py:49
  122.6 222.4 %all-reduce.7.cloned.1.call-start = ((), (), s32[]{:S(2)}) async-start(), calls=%async_computation.1 | async-start | bytes 1638400 | tf_op jit(solution)/shard_map/psum | solution.py:49
  165.0 3.2 collective-permute-start.2
  261.8 2.2 collective-permute-start.3
  266.3 183.1 %all-reduce.9.cloned.1.call-start = ((), (), s32[]{:S(2)}) async-start(), calls=%async_computation.2 | async-start | bytes 1638400 | tf_op jit(solution)/shard_map/psum | solution.py:49
  366.2 2.2 collective-permute-start.4
  370.7 183.1 %all-reduce.11.cloned.1.call-start = ((), (), s32[]{:S(2)}) async-start(), calls=%async_computation.3 | async-start | bytes 1638400 | tf_op jit(solution)/shard_map/psum | solution.py:49
  470.5 2.2 collective-permute-start.5
Sparse Core Ops, SparseCore 0:
  12.5 47.5 all-gather.6
  67.1 44.5 all-gather.8
  118.8 44.5 all-gather.10
  166.8 73.8 all-reduce.4
  266.4 78.5 all-reduce.6
  370.8 78.5 all-reduce.8
  475.1 78.6 all-reduce.10
